TPU v7x, 256 devices: a whole 4x4x8 slice. The times are simulated.
256 devices in a mesh: pole: 8 (over x, core), row: 4 (over z_lo), col: 8 (over z_hi, y).
Axes of the slice: x: 4, y: 4, z: 8 (z_hi: 2, z_lo: 4; z = z_hi * 4 + z_lo), core: 2. Of those that a mesh axis runs over, the one named last changes fastest.
Arguments:
- anc_inverse: bfloat16 [8, 2, 4, 768, 3072], P('pole', None, None, 'col', 'row'), may hold values from -6 to 6
- panel: bfloat16 [8, 2, 3072, 4096], P('pole', None, ('row', 'col')), may hold values from -0.109375 to 0.109375
- pattern: int32 [32, 8], replicated, may hold values 0 or 1
- diag_inverse: bfloat16 [8, 2, 4096, 512], P('pole', None, 'col', 'row'), may hold values from -6 to 6
- pole_weights: float32 [8, 2], P('pole'), may hold values from -4 to 4
Outputs:
- inv_panel: float32 [8, 2, 3072, 4096], P('pole', None, 'row', 'col')
- inv_diag: bfloat16 [8, 2, 4096, 512], P('pole', None, 'col', 'row')
- density: float32 [4096, 512], P('col', 'row')
All inputs are finite; a program needn't handle non-finite values.
Results may differ from a plain program's by a relative error of at most 0.013.
Values may be sent and summed in bfloat16 or wider, within the bound.
A program may use at most 128 MiB of HBM per device.

v0:
```python
import jax
import jax.numpy as jnp
from jax import lax
from jax.sharding import PartitionSpec as P


def in_blocks(shard, dim, length):
    shape = shard.shape
    tiles = shard.reshape(*shape[:dim], length, shape[dim] // length, *shape[dim + 1 :])
    return jnp.moveaxis(tiles, dim, 0)


def sum_at_owner(shard, axis, dim):
    tiles = in_blocks(shard, dim, lax.axis_size(axis))
    arrived = lax.all_to_all(tiles, axis, split_axis=0, concat_axis=0, tiled=True)
    return arrived.sum(axis=0)


def sent_to_all(shard, axis):
    length = lax.axis_size(axis)
    return lax.all_to_all(
        jnp.broadcast_to(shard[None], (length, *shard.shape)), axis, 0, 0, tiled=True
    )


def of_everyone(shard, axis):
    return sent_to_all(shard, axis).astype(jnp.float32).sum(axis=0)


def complex_left(left_re, left_im, right_re, right_im):
    upper = jnp.concatenate([left_re, left_im], axis=1)
    lower = jnp.concatenate([-left_im, left_re], axis=1)
    left_side = jnp.concatenate([upper, lower], axis=0)
    right_side = jnp.concatenate([right_re, right_im], axis=0)
    product = lax.dot_general(
        left_side, right_side, (((0,), (0,)), ((), ())), preferred_element_type=jnp.float32
    )
    return product.reshape(2, left_re.shape[1], right_re.shape[1])


def body(anc_inverse, panel, pattern, diag_inverse, pole_weights):
    n_row = lax.axis_size("row")
    n_col = lax.axis_size("col")
    fine_block = lax.axis_index("row") * n_col + lax.axis_index("col")
    pattern_row = lax.dynamic_slice_in_dim(pattern, fine_block, 1, 0)
    block_rows = panel.shape[2]
    width_all = panel.shape[3]
    groups = pattern.shape[1]
    keep_mask = pattern_row.astype(jnp.bfloat16).reshape(1, 1, 1, groups, 1)
    masked = (panel.reshape(1, 2, block_rows, groups, width_all // groups) * keep_mask).reshape(
        1, 2, block_rows, width_all
    )
    local_rows = lax.all_to_all(masked, "col", split_axis=3, concat_axis=2, tiled=True)
    row_count = anc_inverse.shape[4]
    col_count = local_rows.shape[3]
    full_cols = lax.all_gather(local_rows, "row", axis=2, tiled=True)
    stacked = full_cols[0].reshape(2, n_row, block_rows * n_col, col_count)
    segment = lax.all_gather(anc_inverse, "col", axis=3, tiled=True)
    length = segment.shape[3]
    left_side = segment[0].reshape(2, n_row * length, row_count)
    right_side = stacked.reshape(2, n_row * length, col_count)
    summed = complex_left(left_side[0], left_side[1], right_side[0], right_side[1])
    result_panel = -summed
    rounded = result_panel.astype(jnp.bfloat16)
    diag_terms = complex_left(local_rows[0, 0], local_rows[0, 1], rounded[0], rounded[1])
    row_share = sum_at_owner(diag_terms, "row", 2)
    inverse_diag = diag_inverse[0].astype(jnp.float32) - row_share
    pole_weight = pole_weights[0]
    density_term = pole_weight[0] * inverse_diag[1] + pole_weight[1] * inverse_diag[0]
    density = of_everyone(density_term.astype(jnp.bfloat16), "pole").astype(jnp.float32)
    return (result_panel[None], inverse_diag.astype(jnp.bfloat16)[None], density)


def solution(mesh):
    placed = (
        P("pole", None, None, "col", "row"),
        P("pole", None, ("row", "col"), None),
        P(),
        P("pole", None, "col", "row"),
        P("pole", None),
    )
    return jax.shard_map(
        body,
        mesh=mesh,
        in_specs=placed,
        out_specs=(P("pole", None, "row", "col"), P("pole", None, "col", "row"), P("col", "row")),
        check_vma=False,
    )
```

profile of v0, /device:TPU:105, one launch (start us, length us, event | category | flops | bytes accessed | tf_op | source)
XLA Modules:
  0.0 513.2 jit_solution(11709800237550037159)
XLA Ops:
  7.2 0.0 all-gather.5.cloned.1.call-start
  7.2 0.9 fusion.30
  8.1 0.1 broadcast_bitcast_fusion
  8.2 2.7 broadcast_multiply_fusion
  10.8 5.2 %copy.17 = bf16[1,2,96,4096]{2,1,0,3:T(2,128)(2,1)S(1)} copy(bf16[1,2,96,4096]{3,2,1,0:T(8,128)(2,1)} %broadcast_multiply_fusion) | data formatting | bytes 3145728 | tf_op jit(solution)/shard_map/mul | solution.py:50
  16.0 41.8 %all_to_all.28 = bf16[1,2,96,4096]{2,1,0,3:T(2,128)(2,1)} all-to-all(bf16[1,2,96,4096]{2,1,0,3:T(2,128)(2,1)S(1)} %copy.17), channel_id=1, replica_groups=mesh['pole'=8,'row'=4,'col'=8] {'col'}, dimensions={3} | all-to-all | bytes 3145728 | tf_op jit(solution)/shard_map/all_to_all | solution.py:53
  57.8 6.0 %copy.22 = bf16[1,2,96,8,512]{4,2,3,1,0:T(8,128)(2,1)} copy(bf16[1,2,96,8,512]{2,1,4,3,0:T(2,128)(2,1)} %bitcast.39) | data formatting | bytes 3145728 | tf_op jit(solution)/shard_map/all_to_all | solution.py:53
  63.8 0.0 all-gather.5.cloned.1.call-update
  63.9 0.0 all-gather.3.cloned.1.call-start
  63.9 0.7 all-gather.3.cloned.1.call-update
  64.6 2.1 fusion.33
  66.7 1.3 slice_bitcast_fusion.2
  67.9 128.9 %all-gather.5.cloned.1.call-done = bf16[1,2,3072,512]{3,2,1,0:T(8,128)(2,1)} async-done(((bf16[1,2,768,512]{3,2,1,0:T(8,128)(2,1)}), bf16[1,2,3072,512]{3,2,1,0:T(8,128)(2,1)}) %all-gather.5.cloned.1.call-update) | async-done | bytes 6291472 | tf_op jit(solution)/shard_map/all_gather | solution.py:56
  196.8 4.9 slice_bitcast_fusion.1
  201.8 175.5 %all-gather.3.cloned.1.call-done = bf16[1,2,4,768,768]{4,3,2,1,0:T(8,128)(2,1)} async-done(((bf16[1,2,4,96,768]{4,3,2,1,0:T(8,128)(2,1)}), bf16[1,2,4,768,768]{4,3,2,1,0:T(8,128)(2,1)}) %all-gather.3.cloned.1.call-update) | async-done | bytes 9437200 | tf_op jit(solution)/shard_map/all_gather | solution.py:58
  377.3 6.6 %fusion.34 = (bf16[1,1,4,768,768]{4,3,2,1,0:T(8,128)(2,1)S(1)}, bf16[1,1,4,768,768]{4,3,2,1,0:T(8,128)(2,1)}) fusion(bf16[1,2,4,768,768]{4,3,2,1,0:T(8,128)(2,1)} %all-gather.3.cloned.1.call-done), kind=kLoop, calls=%fused_computation.44 | loop fusion | bytes 18874368 | tf_op jit(solution)/shard_map/slice | solution.py:62
  383.9 3.1 bitcast_negate_fusion
  386.9 0.6 copy-done.1
  387.5 24.3 %fusion.11 = f32[1536,512]{1,0:T(8,128)} fusion(bf16[3072,512]{1,0:T(8,128)(2,1)} %get-tuple-element.6, bf16[3072,512]{1,0:T(8,128)(2,1)S(1)} %get-tuple-element.5, bf16[3072,768]{1,0:T(8,128)(2,1)} %bitcast.41, bf16[3072,768]{1,0:T(8,128)(2,1)} %bitcast_negate_fusion, bf16[3072,768]{1,0:T(8,128)(2,1)} %bitcast.38), kind=kOutput, calls=%fused_computation.11 | convolution fusion | flops 9752543232 | bytes 23592960 | tf_op jit(solution)/shard_map/dot_general | solution.py:35
  411.8 6.0 %fusion.16 = f32[1024,512]{1,0:T(8,128)} fusion(bf16[768,512]{1,0:T(8,128)(2,1)} %get-tuple-element.8, bf16[768,512]{1,0:T(8,128)(2,1)} %fusion.33, bf16[768,512]{1,0:T(8,128)(2,1)} %get-tuple-element.7, f32[1536,512]{1,0:T(8,128)} %fusion.11), kind=kOutput, calls=%fused_computation.14 | convolution fusion | flops 1623982080 | bytes 7602176 | tf_op jit(solution)/shard_map/dot_general | solution.py:35
  417.8 1.9 reshape_reshape.3
  419.8 1.5 copy.25
  421.3 15.3 %all-to-all-start.1 = ((f32[4,2,512,128]{3,2,1,0:T(8,128)}), f32[4,2,512,128]{3,2,1,0:T(8,128)S(1)}, u32[]{:S(2)}, u32[]{:S(2)}) async-start(f32[4,2,512,128]{3,2,1,0:T(8,128)} %bitcast.40), calls=%async_computation.1 | async-start | bytes 4194304 | tf_op jit(solution)/shard_map/all_to_all | solution.py:15
  436.6 0.6 fusion.35
  437.1 44.2 %all-to-all-done.1 = f32[4,2,512,128]{3,2,1,0:T(8,128)S(1)} async-done(((f32[4,2,512,128]{3,2,1,0:T(8,128)}), f32[4,2,512,128]{3,2,1,0:T(8,128)S(1)}, u32[]{:S(2)}, u32[]{:S(2)}) %all-to-all-start.1) | async-done | bytes 2097184 | tf_op jit(solution)/shard_map/all_to_all | solution.py:15
  481.3 0.1 reduce_sum.20
  481.5 1.3 fusion.29
  482.9 1.1 broadcast_in_dim.5
  484.0 6.6 %all-to-all-start.2 = ((bf16[8,512,128]{2,1,0:T(8,128)(2,1)}), bf16[8,512,128]{2,1,0:T(8,128)(2,1)S(1)}, u32[]{:S(2)}, u32[]{:S(2)}) async-start(bf16[8,512,128]{2,1,0:T(8,128)(2,1)} %broadcast_in_dim.5), calls=%async_computation.2 | async-start | bytes 2097152 | tf_op jit(solution)/shard_map/all_to_all | solution.py:21
  490.5 0.8 fusion.25
  491.3 14.2 %all-to-all-done.2 = bf16[8,512,128]{2,1,0:T(8,128)(2,1)S(1)} async-done(((bf16[8,512,128]{2,1,0:T(8,128)(2,1)}), bf16[8,512,128]{2,1,0:T(8,128)(2,1)S(1)}, u32[]{:S(2)}, u32[]{:S(2)}) %all-to-all-start.2) | async-done | bytes 1048608 | tf_op jit(solution)/shard_map/all_to_all | solution.py:21
  505.5 0.8 convert_reduce_fusion
  (9 shorter events, 0.1 us)
Async XLA Ops:
  7.2 189.7 %all-gather.5.cloned.1.call-start = ((), (), s32[]{:S(2)}) async-start(), calls=%async_computation.4 | async-start | bytes 7864320 | tf_op jit(solution)/shard_map/all_gather | solution.py:56
  63.8 2.8 copy-start
  63.9 313.4 %all-gather.3.cloned.1.call-start = ((), (), s32[]{:S(2)}) async-start(), calls=%async_computation.3 | async-start | bytes 10616832 | tf_op jit(solution)/shard_map/all_gather | solution.py:58
  383.9 3.7 copy-start.1
  419.8 16.8 %copy-start.3 = (f32[1,2]{1,0:T(1,128)S(1)}, f32[1,2]{1,0:T(1,128)}, u32[]{:S(2)}) copy-start(f32[1,2]{1,0:T(1,128)} %param.9) | copy-start | bytes 28
  419.8 61.7 %copy-start.2 = (bf16[1,2,512,128]{3,2,1,0:T(8,128)(2,1)S(1)}, bf16[1,2,512,128]{3,2,1,0:T(8,128)(2,1)}, u32[]{:S(2)}) copy-start(bf16[1,2,512,128]{3,2,1,0:T(8,128)(2,1)} %param.8) | copy-start | bytes 786436
  421.3 60.1 %all-to-all-start.1 = ((f32[4,2,512,128]{3,2,1,0:T(8,128)}), f32[4,2,512,128]{3,2,1,0:T(8,128)S(1)}, u32[]{:S(2)}, u32[]{:S(2)}) async-start(f32[4,2,512,128]{3,2,1,0:T(8,128)} %bitcast.40), calls=%async_computation.1 | async-start | bytes 4194304 | tf_op jit(solution)/shard_map/all_to_all | solution.py:15
  484.0 21.5 %all-to-all-start.2 = ((bf16[8,512,128]{2,1,0:T(8,128)(2,1)}), bf16[8,512,128]{2,1,0:T(8,128)(2,1)S(1)}, u32[]{:S(2)}, u32[]{:S(2)}) async-start(bf16[8,512,128]{2,1,0:T(8,128)(2,1)} %broadcast_in_dim.5), calls=%async_computation.2 | async-start | bytes 2097152 | tf_op jit(solution)/shard_map/all_to_all | solution.py:21
Sparse Core Ops, SparseCore 0:
  64.0 132.8 all-gather.4
  199.4 177.8 all-gather.2
where the time goes:
time: 519 us; the launch traced here: 513 us
  waiting for transfers between devices  363 us (70%)
  blocking collectives  41.8 us (8%)
  matrix products  30.3 us (6%)
  local copies, waits for them, and re-layouts  29.7 us (6%)
  starting transfers between devices  22 us (4%)
  between operations  14.1 us (3%)
  other arithmetic  11.8 us (2%)
    all_gather x1, waiting for transfers between devices, body(): segment = lax.all_gather(anc_inverse, 'col', axis=3, tiled=True)  176 us
    all_gather x1, waiting for transfers between devices, body(): full_cols = lax.all_gather(local_rows, 'row', axis=2, tiled=True)  129 us
    all_to_all x1, waiting for transfers between devices, sum_at_owner(): lax.all_to_all(tiles, axis, split_axis=0, concat_axis=0, tiled=True)  44.2 us
    all_to_all x1, blocking collectives, body(): lax.all_to_all(masked, 'col', split_axis=3, concat_axis=2, tiled=True)  41.8 us
    dot_general x2, matrix products, complex_left(): lax.dot_general(left_side, right_side, (((0,), (0,)), ((), ())), preferre...  30.3 us
    all_to_all x1, starting transfers between devices, sum_at_owner(): lax.all_to_all(tiles, axis, split_axis=0, concat_axis=0, tiled=True)  15.3 us
    all_to_all x1, waiting for transfers between devices, sent_to_all(): lax.all_to_all(jnp.broadcast_to(shard[None], (length, *shard.shape)), axi...  14.2 us
  transfers between devices with their start and end apart: 4, of which 4 were waited for; matrix products, arithmetic and copies ran while one was open for 2% of the time, Pallas kernels for 0%

commit v1 on v0

v1 whole, which is shorter than its diff:
```python
import jax
import jax.numpy as jnp
from jax import lax
from jax.experimental import pallas as pl
from jax.experimental.pallas import tpu as pltpu
from jax.sharding import PartitionSpec as P

MESH = pl.DeviceIdType.MESH
F32 = jnp.float32
BF16 = jnp.bfloat16

E = 96
ROWS = 768
LN = 128
ORDER = (0, 3, 1, 2)


def copy_to(src, dst, send_sem, recv_sem, dev):
    return pltpu.make_async_remote_copy(
        src_ref=src,
        dst_ref=dst,
        send_sem=send_sem,
        recv_sem=recv_sem,
        device_id=dev,
        device_id_type=MESH,
    )


def dot(a, b, dims=(1, 0)):
    return lax.dot_general(
        a, b, (((dims[0],), (dims[1],)), ((), ())), preferred_element_type=F32
    )


def kernel(
    pat, wgt, g_in, p_in, d_in,
    x_out, id_out, den_out,
    gbuf, gt, lsrc, lbuf, loth, lrel, acc, xs, xb, dsend, drecv, term, tpair, px, dh, dp,
    a_s, a_r, gz_s, gz_r, gy_s, gy_r, gr_s, gr_r, gc_s, gc_r,
    lp_s, lp_r, lm_s, lm_r, x_s, x_r, d_s, d_r, t_s, t_r, p_s, p_r, h_s, h_r, o_s,
):
    pole = lax.axis_index("pole")
    r = lax.axis_index("row")
    c = lax.axis_index("col")
    h = c // 4
    y = lax.rem(c, 4)
    z = 4 * h + r
    oth = 1 - h
    core = lax.rem(pole, 2)
    xx = pole // 2

    def at_y(d):
        return {"col": 4 * h + lax.rem(y + d, 4)}

    def at_z(d):
        zz = lax.rem(z + d, 8)
        return {"row": lax.rem(zz, 4), "col": (zz // 4) * 4 + y}

    def at_row(d):
        return {"row": lax.rem(r + d, 4)}

    def at_x(d):
        return {"pole": lax.rem(xx + d, 4) * 2 + core}

    partner = {"pole": 2 * xx + 1 - core}
    across = {"col": 4 * oth + y}

    bar = pltpu.get_barrier_semaphore()
    peers = [at_y(1), at_y(2), at_y(3), at_z(1), at_z(7), across, partner]
    peers += [at_row(d) for d in (1, 2, 3)] + [at_x(d) for d in (1, 2, 3)]
    for dev in peers:
        pl.semaphore_signal(bar, inc=1, device_id=dev, device_id_type=MESH)
    pl.semaphore_wait(bar, len(peers))

    def gz(t):
        return copy_to(g_in.at[0, t], gbuf.at[h, t, :, y], gz_s.at[t], gz_r.at[t], across)

    for t in (0, 1):
        gz(t).start()

    fine = r * 8 + c
    for k in range(8):
        keep = pat[fine, k].astype(F32)
        for j in range(4):
            lo = k * 512 + ORDER[j] * LN
            for t in (0, 1):
                blk = p_in[0, t, :, lo:lo + LN].astype(F32) * keep
                lsrc[k, j, :, t * LN:(t + 1) * LN] = blk.astype(BF16)
    gbuf[h, :, :, y] = g_in[0]

    def to_col(d, which):
        k = (h if which == 0 else oth) * 4 + lax.rem(y + d, 4)
        dst = lbuf.at[:, z, y] if which == 0 else loth.at[:, y]
        return copy_to(lsrc.at[k], dst, a_s.at[d - 1, which], a_r.at[d - 1, which], at_y(d))

    for which in (1, 0):
        for d in (1, 3, 2):
            to_col(d, which).start()

    def gy(way, t):
        return copy_to(
            g_in.at[0, t], gbuf.at[h, t, :, y], gy_s.at[way, t], gy_r.at[way, t], at_y(1 if way == 0 else 3)
        )

    for i in (0, 1):
        gy(0, i).start()
        gy(1, 1 - i).start()

    lbuf[:, z, y] = lsrc[h * 4 + y]
    loth[:, y] = lsrc[oth * 4 + y]

    for which in (1, 0):
        for d in (1, 3, 2):
            to_col(d, which).wait_recv()

    def up(j, i, src, zp):
        return copy_to(src, lbuf.at[j, zp], lp_s.at[j, i], lp_r.at[j, i], at_z(1))

    def down(j, i, src, zp):
        return copy_to(src, lbuf.at[j, zp], lm_s.at[j, i], lm_r.at[j, i], at_z(7))

    def extra(j, d):
        return copy_to(loth.at[j], lrel.at[j], x_s.at[j], x_r.at[j], at_z(d))

    @pl.loop(0, 4)
    def _(j):
        @pl.when(r == 2)
        def _():
            extra(j, 1).start()

        @pl.when(r == 1)
        def _():
            extra(j, 7).start()

        @pl.when(r == 3)
        def _():
            up(j, 1, loth.at[j], z).start()

        @pl.when(r == 0)
        def _():
            down(j, 1, loth.at[j], z).start()

    @pl.loop(0, 4)
    def _(j):
        @pl.when(r < 3)
        def _():
            up(j, r + 2, lbuf.at[j, z], z).start()

        @pl.when(r > 0)
        def _():
            down(j, 5 - r, lbuf.at[j, z], z).start()

    def relay(way):
        t = way
        frm = lax.rem(y + (3 if way == 0 else 1), 4)
        ref = gbuf.at[h, t, :, frm]
        return copy_to(ref, ref, gr_s.at[way], gr_r.at[way], at_y(1 if way == 0 else 3))

    gy(0, 0).wait_recv()
    relay(0).start()
    gy(1, 1).wait_recv()
    relay(1).start()

    def gc(d, t):
        ref = gbuf.at[oth, t, :, y]
        return copy_to(ref, ref, gc_s.at[d - 1, t], gc_r.at[d - 1, t], at_y(d))

    for t in (0, 1):
        gz(t).wait_recv()
        for d in (1, 3, 2):
            gc(d, t).start()

    @pl.loop(0, 4)
    def _(j):
        @pl.when(r == 3)
        def _():
            extra(j, 1).wait_recv()
            up(j, 0, lrel.at[j], 4 * h + 2).start()

        @pl.when(r == 0)
        def _():
            extra(j, 7).wait_recv()
            down(j, 0, lrel.at[j], 4 * h + 1).start()

    gy(0, 1).wait_recv()
    gy(1, 0).wait_recv()
    relay(0).wait_recv()
    relay(1).wait_recv()

    def turn(half):
        @pl.loop(0, 4)
        def _(q):
            for t in (0, 1):
                gt[half * 4 + q, t] = gbuf[half, t, q].reshape(4 * E, ROWS).T

    turn(h)

    def compute(slot, j, zp):
        right = lbuf[j, zp].reshape(4 * E, 2 * LN)
        for t in (0, 1):
            acc[slot, t] += dot(gt[zp, t], right)

    def first(slot, j):
        right = lbuf[j, z].reshape(4 * E, 2 * LN)
        for t in (0, 1):
            acc[slot, t] = dot(gt[z, t], right)

    def stream(j, work):
        for slot, jj in work:
            first(slot, jj)

        @pl.loop(0, 5)
        def _(i):
            zp = lax.rem(4 * h + 6 + i, 8)
            zm = lax.rem(4 * h + 5 - i + 8, 8)

            @pl.when(i < r + 2)
            def _():
                one = up(j, i, lbuf.at[j, zp], zp)
                one.wait_recv()

                @pl.when(r < 3)
                def _():
                    one.start()

            @pl.when(i < 5 - r)
            def _():
                one = down(j, i, lbuf.at[j, zm], zm)
                one.wait_recv()

                @pl.when(r > 0)
                def _():
                    one.start()

            @pl.when(i < r + 2)
            def _():
                for slot, jj in work:
                    compute(slot, jj, zp)

            @pl.when(i < 5 - r)
            def _():
                for slot, jj in work:
                    compute(slot, jj, zm)

    def out_copy(j):
        cols = pl.ds(ORDER[j] * LN, LN)
        return pltpu.make_async_copy(xs.at[:, :, cols], x_out.at[0, :, :, cols], o_s.at[j])

    def finish(slot, j):
        lo = ORDER[j] * LN

        @pl.loop(0, 8)
        def _(b):
            rows = pl.ds(b * E, E)
            re = acc[slot, 1, rows, LN:] - acc[slot, 0, rows, :LN]
            im = -(acc[slot, 0, rows, LN:] + acc[slot, 1, rows, :LN])
            xs[0, rows, lo:lo + LN] = re
            xs[1, rows, lo:lo + LN] = im
            xb[j, rows, :LN] = re.astype(BF16)
            xb[j, rows, LN:] = im.astype(BF16)

        out_copy(j).start()

    def diag(ja, jb):
        low = lbuf[ja, r].reshape(4 * E, 2 * LN)
        high = lbuf[ja, 4 + r].reshape(4 * E, 2 * LN)
        both = dot(low, xb[jb, :4 * E], (0, 0)) + dot(high, xb[jb, 4 * E:], (0, 0))
        lo = ORDER[ja] * LN
        dsend[ORDER[jb], 0, lo:lo + LN] = (both[:LN, :LN] - both[LN:, LN:]).astype(BF16)
        dsend[ORDER[jb], 1, lo:lo + LN] = (both[:LN, LN:] + both[LN:, :LN]).astype(BF16)

    stream(0, ())
    for t in (0, 1):
        for d in (1, 3, 2):
            gc(d, t).wait_recv()
    turn(oth)
    stream(1, ((0, 0),))
    finish(0, 0)
    stream(2, ((1, 1),))
    finish(1, 1)
    stream(3, ((0, 2), (1, 3)))
    finish(0, 2)
    finish(1, 3)

    for jb in range(4):
        for ja in range(4):
            diag(ja, jb)

    def share(d):
        return copy_to(
            dsend.at[lax.rem(r + d, 4)], drecv.at[d - 1], d_s.at[d - 1], d_r.at[d - 1], at_row(d)
        )

    for d in (1, 2, 3):
        share(d).start()
    for d in (1, 2, 3):
        share(d).wait_recv()

    def full(t):
        got = dsend[r, t].astype(F32)
        for d in range(3):
            got += drecv[d, t].astype(F32)
        return d_in[0, t].astype(F32) - got

    re = full(0)
    im = full(1)
    id_out[0, 0] = re.astype(BF16)
    id_out[0, 1] = im.astype(BF16)
    term[...] = wgt[0, 0] * im + wgt[0, 1] * re

    mine = pl.ds(pl.multiple_of(core * 256, 256), 256)
    other = pl.ds(pl.multiple_of((1 - core) * 256, 256), 256)
    pair = copy_to(term.at[other], tpair, t_s, t_r, partner)
    pair.start()
    pair.wait_recv()
    px[xx] = (term[mine, :] + tpair[...]).astype(BF16)

    def along(d):
        return copy_to(px.at[xx], px.at[xx], p_s.at[d - 1], p_r.at[d - 1], at_x(d))

    for d in (1, 3, 2):
        along(d).start()
    for d in (1, 3, 2):
        along(d).wait_recv()
    half = px[0].astype(F32)
    for k in range(1, 4):
        half += px[k].astype(F32)
    dh[...] = half
    den_out[mine, :] = half
    swap = copy_to(dh, dp, h_s, h_r, partner)
    swap.start()
    swap.wait_recv()
    den_out[other, :] = dp[...]

    for t in (0, 1):
        gz(t).wait_send()
        gy(0, t).wait_send()
        gy(1, t).wait_send()
        relay(t).wait_send()
        for d in (1, 2, 3):
            gc(d, t).wait_send()
            to_col(d, t).wait_send()
    for d in (1, 2, 3):
        share(d).wait_send()
        along(d).wait_send()
    pair.wait_send()
    swap.wait_send()

    @pl.loop(0, 4)
    def _(j):
        @pl.when((r == 1) | (r == 2))
        def _():
            extra(j, 1).wait_send()

        @pl.loop(0, 5)
        def _(i):
            @pl.when(((r < 3) & (i < r + 3)) | ((r == 3) & (i < 2)))
            def _():
                up(j, i, lbuf.at[j, z], z).wait_send()

            @pl.when(((r > 0) & (i < 6 - r)) | ((r == 0) & (i < 2)))
            def _():
                down(j, i, lbuf.at[j, z], z).wait_send()

    for j in range(4):
        out_copy(j).wait()


def body(anc_inverse, panel, pattern, diag_inverse, pole_weights):
    vmem = pl.BlockSpec(memory_space=pltpu.VMEM)
    smem = pl.BlockSpec(memory_space=pltpu.SMEM)
    dma = pltpu.SemaphoreType.DMA
    sems = [(3, 2), (2,), (2, 2), (2,), (3, 2), (4, 5), (4, 5), (4,), (3,), None, (3,), None]
    pairs = []
    for shape in sems:
        one = dma if shape is None else dma(shape)
        pairs += [one, one]
    return pl.pallas_call(
        kernel,
        out_shape=(
            jax.ShapeDtypeStruct((1, 2, ROWS, 512), F32),
            jax.ShapeDtypeStruct((1, 2, 512, LN), BF16),
            jax.ShapeDtypeStruct((512, LN), F32),
        ),
        in_specs=[smem, smem, vmem, vmem, vmem],
        out_specs=(pl.BlockSpec(memory_space=pl.ANY), vmem, vmem),
        scratch_shapes=[
            pltpu.VMEM((2, 2, 4, 4, E, ROWS), BF16),
            pltpu.VMEM((8, 2, ROWS, 4 * E), BF16),
            pltpu.VMEM((8, 4, E, 2 * LN), BF16),
            pltpu.VMEM((4, 8, 4, E, 2 * LN), BF16),
            pltpu.VMEM((4, 4, E, 2 * LN), BF16),
            pltpu.VMEM((4, 4, E, 2 * LN), BF16),
            pltpu.VMEM((2, 2, ROWS, 2 * LN), F32),
            pltpu.VMEM((2, ROWS, 512), F32),
            pltpu.VMEM((4, ROWS, 2 * LN), BF16),
            pltpu.VMEM((4, 2, 512, LN), BF16),
            pltpu.VMEM((3, 2, 512, LN), BF16),
            pltpu.VMEM((512, LN), F32),
            pltpu.VMEM((256, LN), F32),
            pltpu.VMEM((4, 256, LN), BF16),
            pltpu.VMEM((256, LN), F32),
            pltpu.VMEM((256, LN), F32),
            *pairs,
            dma((4,)),
        ],
        compiler_params=pltpu.CompilerParams(
            collective_id=0, has_side_effects=True, vmem_limit_bytes=60 * 1024 * 1024
        ),
    )(pattern, pole_weights, anc_inverse, panel, diag_inverse)


def solution(mesh):
    placed = (
        P("pole", None, None, "col", "row"),
        P("pole", None, ("row", "col"), None),
        P(),
        P("pole", None, "col", "row"),
        P("pole", None),
    )
    return jax.shard_map(
        body,
        mesh=mesh,
        in_specs=placed,
        out_specs=(P("pole", None, "row", "col"), P("pole", None, "col", "row"), P("col", "row")),
        check_vma=False,
    )
```

time: 519 us -> 426 us (0.82); the launches traced: 513 us -> 426 us
  Pallas kernels: 0 us -> 418 us
  waiting for transfers between devices: 363 us -> 0 us
  blocking collectives: 41.8 us -> 0 us
  matrix products: 30.3 us -> 0 us
  local copies, waits for them, and re-layouts: 29.7 us -> 6.69 us
  starting transfers between devices: 22 us -> 0 us
  between operations: 14.1 us -> 0.66 us
  other arithmetic: 11.8 us -> 0 us
    pallas_call x0 -> x1, Pallas kernels: none -> 418 us  [body(): pl.pallas_call(kernel, out_shape=(jax.ShapeDtypeStruct((1, 2, ROWS, 512),...]
    all_gather x2 -> x0, waiting for transfers between devices: 304 us -> none  [the longest x1 176 us: body(): segment = lax.all_gather(anc_inverse, 'col', axis=3, tiled=True)]
    all_to_all x2 -> x0, waiting for transfers between devices: 58.4 us -> none  [the longest x1 44.2 us: sum_at_owner(): lax.all_to_all(tiles, axis, split_axis=0, concat_axis=0, tiled=True)]
    all_to_all x1 -> x0, blocking collectives: 41.8 us -> none  [body(): lax.all_to_all(masked, 'col', split_axis=3, concat_axis=2, tiled=True)]
    dot_general x2 -> x0, matrix products: 30.3 us -> none  [complex_left(): lax.dot_general(left_side, right_side, (((0,), (0,)), ((), ())), preferre...]
    all_to_all x2 -> x0, starting transfers between devices: 21.9 us -> none  [the longest x1 15.3 us: sum_at_owner(): lax.all_to_all(tiles, axis, split_axis=0, concat_axis=0, tiled=True)]
    slice x2 -> x0, local copies, waits for them, and re-layouts: 7.19 us -> none  [the longest x1 6.61 us: body(): left_side[1]]
    squeeze x2 -> x0, local copies, waits for them, and re-layouts: 6.18 us -> none  [the longest x1 4.91 us: body(): right_side[0]]
  transfers between devices with their start and end apart: 4 -> 0, of which waited for: 4 -> 0; matrix products, arithmetic and copies ran while one was open for 2% -> 0% of each run, Pallas kernels for 0% -> 0%
where the time goes in v1:
time: 426 us
  Pallas kernels  418 us (98%)
  local copies, waits for them, and re-layouts  6.69 us (2%)
    pallas_call x1, Pallas kernels, body(): pl.pallas_call(kernel, out_shape=(jax.ShapeDtypeStruct((1, 2, ROWS, 512),...  418 us

profile of v1, /device:TPU:105, one launch (start us, length us, event | category | flops | bytes accessed | tf_op | source)
XLA Modules:
  0.0 425.8 jit_solution(8500871414499495191)
XLA Ops:
  0.6 1.4 copy.8.pat
  2.0 418.4 %shard_map.76 = (f32[1,2,768,512]{3,2,1,0:T(8,128)}, bf16[1,2,512,128]{3,2,1,0:T(8,128)(2,1)}, f32[512,128]{1,0:T(8,128)}) custom-call(s32[32,8]{1,0:T(8,128)} %copy.8.pat, f32[1,2]{1,0:T(1,128)} %wgt.1, bf16[1,2,4,96,768]{4,3,2,1,0:T(8,128)(2,1)} %g_in.1, bf16[1,2,96,4096]{3,2,1,0:T(8,128)(2,1)} %p_in.1, bf16[1,2,512,128]{3,2,1,0:T(8,128)(2,1)} %d_in.1), custom_call_target="tpu_custom_call" | custom-call | tf_op jit(solution)/shard_map/pallas_call | solution.py:378
  420.5 0.0 copy-start.1
  420.5 0.0 copy-start
  420.5 3.9 copy.12
  424.4 0.0 copy-done.1
  424.4 0.7 copy.13
  425.1 0.0 copy-done
  425.1 0.7 copy.14
Async XLA Ops:
  420.5 3.9 copy-start.1
  420.5 4.6 %copy-start = (f32[512,128]{1,0:T(8,128)S(1)}, f32[512,128]{1,0:T(8,128)}, u32[]{:S(2)}) copy-start(f32[512,128]{1,0:T(8,128)} %get-tuple-element.8) | copy-start | bytes 786436

commit v2 on v1

--- a/solution.py
+++ b/solution.py
@@ -80,7 +80,7 @@
 
     fine = r * 8 + c
     for k in range(8):
-        keep = pat[fine, k].astype(F32)
+        keep = pat[k, fine].astype(F32)
         for j in range(4):
             lo = k * 512 + ORDER[j] * LN
             for t in (0, 1):
@@ -122,8 +122,7 @@
     def extra(j, d):
         return copy_to(loth.at[j], lrel.at[j], x_s.at[j], x_r.at[j], at_z(d))
 
-    @pl.loop(0, 4)
-    def _(j):
+    def launch(j):
         @pl.when(r == 2)
         def _():
             extra(j, 1).start()
@@ -134,21 +133,22 @@
 
         @pl.when(r == 3)
         def _():
-            up(j, 1, loth.at[j], z).start()
+            up(j, 0, loth.at[j], z).start()
 
         @pl.when(r == 0)
         def _():
-            down(j, 1, loth.at[j], z).start()
-
-    @pl.loop(0, 4)
-    def _(j):
+            down(j, 0, loth.at[j], z).start()
+
         @pl.when(r < 3)
         def _():
-            up(j, r + 2, lbuf.at[j, z], z).start()
+            up(j, 0, lbuf.at[j, z], z).start()
 
         @pl.when(r > 0)
         def _():
-            down(j, 5 - r, lbuf.at[j, z], z).start()
+            down(j, 0, lbuf.at[j, z], z).start()
+
+    for j in (0, 1):
+        launch(j)
 
     def relay(way):
         t = way
@@ -170,18 +170,6 @@
         for d in (1, 3, 2):
             gc(d, t).start()
 
-    @pl.loop(0, 4)
-    def _(j):
-        @pl.when(r == 3)
-        def _():
-            extra(j, 1).wait_recv()
-            up(j, 0, lrel.at[j], 4 * h + 2).start()
-
-        @pl.when(r == 0)
-        def _():
-            extra(j, 7).wait_recv()
-            down(j, 0, lrel.at[j], 4 * h + 1).start()
-
     gy(0, 1).wait_recv()
     gy(1, 0).wait_recv()
     relay(0).wait_recv()
@@ -200,47 +188,57 @@
         for t in (0, 1):
             acc[slot, t] += dot(gt[zp, t], right)
 
-    def first(slot, j):
+    def first(j):
         right = lbuf[j, z].reshape(4 * E, 2 * LN)
         for t in (0, 1):
-            acc[slot, t] = dot(gt[z, t], right)
-
-    def stream(j, work):
-        for slot, jj in work:
-            first(slot, jj)
-
-        @pl.loop(0, 5)
-        def _(i):
-            zp = lax.rem(4 * h + 6 + i, 8)
-            zm = lax.rem(4 * h + 5 - i + 8, 8)
-
-            @pl.when(i < r + 2)
-            def _():
-                one = up(j, i, lbuf.at[j, zp], zp)
-                one.wait_recv()
-
+            acc[j, t] = dot(gt[z, t], right)
+
+    def edge(j):
+        @pl.when(r == 3)
+        def _():
+            extra(j, 1).wait_recv()
+            up(j, 1, lrel.at[j], 4 * h + 2).start()
+
+        @pl.when(r == 0)
+        def _():
+            extra(j, 7).wait_recv()
+            down(j, 1, lrel.at[j], 4 * h + 1).start()
+
+    def relay_from(j, d):
+        zp = lax.rem(z + 7 - d, 8)
+        zm = lax.rem(z + 1 + d, 8)
+
+        @pl.when(d < r + 2)
+        def _():
+            up(j, d, lbuf.at[j, zp], zp).wait_recv()
+
+            if d < 4:
                 @pl.when(r < 3)
                 def _():
-                    one.start()
-
-            @pl.when(i < 5 - r)
-            def _():
-                one = down(j, i, lbuf.at[j, zm], zm)
-                one.wait_recv()
-
+                    up(j, d + 1, lbuf.at[j, zp], zp).start()
+
+        @pl.when(d < 5 - r)
+        def _():
+            down(j, d, lbuf.at[j, zm], zm).wait_recv()
+
+            if d < 4:
                 @pl.when(r > 0)
                 def _():
-                    one.start()
-
-            @pl.when(i < r + 2)
-            def _():
-                for slot, jj in work:
-                    compute(slot, jj, zp)
-
-            @pl.when(i < 5 - r)
-            def _():
-                for slot, jj in work:
-                    compute(slot, jj, zm)
+                    down(j, d + 1, lbuf.at[j, zm], zm).start()
+
+    def compute_from(j, d):
+        @pl.when(d < r + 2)
+        def _():
+            compute(j, j, lax.rem(z + 7 - d, 8))
+
+        @pl.when(d < 5 - r)
+        def _():
+            compute(j, j, lax.rem(z + 1 + d, 8))
+
+    def compute_rest(j):
+        @pl.loop(1, 8)
+        def _(k):
+            compute(j, j, lax.rem(z + k, 8))
 
     def out_copy(j):
         cols = pl.ds(ORDER[j] * LN, LN)
@@ -269,18 +267,32 @@
         dsend[ORDER[jb], 0, lo:lo + LN] = (both[:LN, :LN] - both[LN:, LN:]).astype(BF16)
         dsend[ORDER[jb], 1, lo:lo + LN] = (both[:LN, LN:] + both[LN:, :LN]).astype(BF16)
 
-    stream(0, ())
+    for d in range(5):
+        for j in (0, 1):
+            if d == 0:
+                edge(j)
+            relay_from(j, d)
+        if d == 2:
+            for j in (2, 3):
+                launch(j)
     for t in (0, 1):
         for d in (1, 3, 2):
             gc(d, t).wait_recv()
     turn(oth)
-    stream(1, ((0, 0),))
-    finish(0, 0)
-    stream(2, ((1, 1),))
-    finish(1, 1)
-    stream(3, ((0, 2), (1, 3)))
-    finish(0, 2)
-    finish(1, 3)
+    for d in range(5):
+        for j in (2, 3):
+            if d == 0:
+                edge(j)
+            relay_from(j, d)
+            if d == 0:
+                first(j)
+            compute_from(j, d)
+        if d < 2:
+            first(d)
+            compute_rest(d)
+            finish(d, d)
+    finish(2, 2)
+    finish(3, 3)
 
     for jb in range(4):
         for ja in range(4):
@@ -391,7 +403,7 @@
             pltpu.VMEM((4, 8, 4, E, 2 * LN), BF16),
             pltpu.VMEM((4, 4, E, 2 * LN), BF16),
             pltpu.VMEM((4, 4, E, 2 * LN), BF16),
-            pltpu.VMEM((2, 2, ROWS, 2 * LN), F32),
+            pltpu.VMEM((4, 2, ROWS, 2 * LN), F32),
             pltpu.VMEM((2, ROWS, 512), F32),
             pltpu.VMEM((4, ROWS, 2 * LN), BF16),
             pltpu.VMEM((4, 2, 512, LN), BF16),
@@ -407,7 +419,7 @@
         compiler_params=pltpu.CompilerParams(
             collective_id=0, has_side_effects=True, vmem_limit_bytes=60 * 1024 * 1024
         ),
-    )(pattern, pole_weights, anc_inverse, panel, diag_inverse)
+    )(pattern.T, pole_weights, anc_inverse, panel, diag_inverse)
 
 
 def solution(mesh):

time: 426 us -> 204 us (0.48)
  Pallas kernels: 418 us -> 197 us
    pallas_call x1, Pallas kernels: 418 us -> 197 us  [body(): pl.pallas_call(kernel, out_shape=(jax.ShapeDtypeStruct((1, 2, ROWS, 512),...]
where the time goes in v2:
time: 204 us; the launch traced here: 203 us
  Pallas kernels  197 us (97%)
  local copies, waits for them, and re-layouts  5.33 us (3%)
    pallas_call x1, Pallas kernels, body(): pl.pallas_call(kernel, out_shape=(jax.ShapeDtypeStruct((1, 2, ROWS, 512),...  197 us
    unnamed x7, local copies, waits for them, and re-layouts  5.33 us

profile of v2, /device:TPU:105, one launch (start us, length us, event | category | flops | bytes accessed | tf_op | source)
XLA Modules:
  0.0 203.2 jit_solution(17542361335945895149)
XLA Ops:
  0.6 197.2 %shard_map.76 = (f32[1,2,768,512]{3,2,1,0:T(8,128)}, bf16[1,2,512,128]{3,2,1,0:T(8,128)(2,1)}, f32[512,128]{1,0:T(8,128)}) custom-call(s32[8,32]{1,0:T(8,128)} %bitcast.1, f32[1,2]{1,0:T(1,128)} %wgt.1, bf16[1,2,4,96,768]{4,3,2,1,0:T(8,128)(2,1)} %g_in.1, bf16[1,2,96,4096]{3,2,1,0:T(8,128)(2,1)} %p_in.1, bf16[1,2,512,128]{3,2,1,0:T(8,128)(2,1)} %d_in.1), custom_call_target="tpu_custom_call" | custom-call | tf_op jit(solution)/shard_map/pallas_call | solution.py:390
  197.9 0.0 copy-start.1
  197.9 0.0 copy-start
  197.9 3.9 %copy.11 = f32[1,2,768,512]{3,2,1,0:T(8,128)} copy(f32[1,2,768,512]{3,2,1,0:T(8,128)} %get-tuple-element.6) | data formatting | bytes 6291456
  201.8 0.0 copy-done.1
  201.8 0.7 copy.12
  202.5 0.0 copy-done
  202.5 0.7 copy.13
Async XLA Ops:
  197.9 3.9 %copy-start.1 = (bf16[1,2,512,128]{3,2,1,0:T(8,128)(2,1)S(1)}, bf16[1,2,512,128]{3,2,1,0:T(8,128)(2,1)}, u32[]{:S(2)}) copy-start(bf16[1,2,512,128]{3,2,1,0:T(8,128)(2,1)} %get-tuple-element.7) | copy-start | bytes 786436
  197.9 4.6 %copy-start = (f32[512,128]{1,0:T(8,128)S(1)}, f32[512,128]{1,0:T(8,128)}, u32[]{:S(2)}) copy-start(f32[512,128]{1,0:T(8,128)} %get-tuple-element.8) | copy-start | bytes 786436

commit v3 on v2

--- a/solution.py
+++ b/solution.py
@@ -12,7 +12,7 @@
 E = 96
 ROWS = 768
 LN = 128
-ORDER = (0, 3, 1, 2)
+ORDER = (1, 2, 0, 3)
 
 
 def copy_to(src, dst, send_sem, recv_sem, dev):
@@ -279,6 +279,17 @@
         for d in (1, 3, 2):
             gc(d, t).wait_recv()
     turn(oth)
+    def share(j):
+        own = ORDER[j]
+        d = lax.rem(own + 4 - r, 4) - 1
+        slot = jnp.maximum(d, 0)
+        return copy_to(dsend.at[own], drecv.at[slot], d_s.at[slot], d_r.at[slot], {"row": own})
+
+    def give(j):
+        @pl.when(r != ORDER[j])
+        def _():
+            share(j).start()
+
     for d in range(5):
         for j in (2, 3):
             if d == 0:
@@ -291,22 +302,27 @@
             first(d)
             compute_rest(d)
             finish(d, d)
+        if d == 2:
+            for jb in (0, 1):
+                for ja in (0, 1):
+                    diag(ja, jb)
+        if d == 3:
+            for jb in (0, 1):
+                for ja in (2, 3):
+                    diag(ja, jb)
+            give(0)
+            give(1)
     finish(2, 2)
+    for ja in range(4):
+        diag(ja, 2)
     finish(3, 3)
-
-    for jb in range(4):
-        for ja in range(4):
-            diag(ja, jb)
-
-    def share(d):
-        return copy_to(
-            dsend.at[lax.rem(r + d, 4)], drecv.at[d - 1], d_s.at[d - 1], d_r.at[d - 1], at_row(d)
-        )
-
-    for d in (1, 2, 3):
-        share(d).start()
-    for d in (1, 2, 3):
-        share(d).wait_recv()
+    give(2)
+    for ja in range(4):
+        diag(ja, 3)
+    give(3)
+
+    for d in range(3):
+        copy_to(dsend.at[r], drecv.at[d], d_s.at[d], d_r.at[d], partner).wait_recv()
 
     def full(t):
         got = dsend[r, t].astype(F32)
@@ -352,8 +368,12 @@
         for d in (1, 2, 3):
             gc(d, t).wait_send()
             to_col(d, t).wait_send()
+    for j in range(4):
+        @pl.when(r != ORDER[j])
+        def _():
+            share(j).wait_send()
+
     for d in (1, 2, 3):
-        share(d).wait_send()
         along(d).wait_send()
     pair.wait_send()
     swap.wait_send()

time: 204 us -> 197 us (0.966); the launches traced: 203 us -> 193 us
  Pallas kernels: 197 us -> 187 us
    pallas_call x1, Pallas kernels: 197 us -> 187 us  [body(): pl.pallas_call(kernel, out_shape=(jax.ShapeDtypeStruct((1, 2, ROWS, 512),...]
where the time goes in v3:
time: 197 us; the launch traced here: 193 us
  Pallas kernels  187 us (95%)
  local copies, waits for them, and re-layouts  5.33 us (3%)
    pallas_call x1, Pallas kernels, body(): pl.pallas_call(kernel, out_shape=(jax.ShapeDtypeStruct((1, 2, ROWS, 512),...  187 us
    unnamed x7, local copies, waits for them, and re-layouts  5.33 us

profile of v3, /device:TPU:105, one launch (start us, length us, event | category | flops | bytes accessed | tf_op | source)
XLA Modules:
  0.0 193.5 jit_solution(17267165952987933722)
XLA Ops:
  0.6 187.5 %shard_map.76 = (f32[1,2,768,512]{3,2,1,0:T(8,128)}, bf16[1,2,512,128]{3,2,1,0:T(8,128)(2,1)}, f32[512,128]{1,0:T(8,128)}) custom-call(s32[8,32]{1,0:T(8,128)} %bitcast.1, f32[1,2]{1,0:T(1,128)} %wgt.1, bf16[1,2,4,96,768]{4,3,2,1,0:T(8,128)(2,1)} %g_in.1, bf16[1,2,96,4096]{3,2,1,0:T(8,128)(2,1)} %p_in.1, bf16[1,2,512,128]{3,2,1,0:T(8,128)(2,1)} %d_in.1), custom_call_target="tpu_custom_call" | custom-call | tf_op jit(solution)/shard_map/pallas_call | solution.py:410
  188.1 0.0 copy-start.1
  188.1 0.0 copy-start
  188.1 3.9 %copy.11 = f32[1,2,768,512]{3,2,1,0:T(8,128)} copy(f32[1,2,768,512]{3,2,1,0:T(8,128)} %get-tuple-element.6) | data formatting | bytes 6291456
  192.1 0.0 copy-done.1
  192.1 0.7 copy.12
  192.8 0.0 copy-done
  192.8 0.7 copy.13
Async XLA Ops:
  188.1 3.9 %copy-start.1 = (bf16[1,2,512,128]{3,2,1,0:T(8,128)(2,1)S(1)}, bf16[1,2,512,128]{3,2,1,0:T(8,128)(2,1)}, u32[]{:S(2)}) copy-start(bf16[1,2,512,128]{3,2,1,0:T(8,128)(2,1)} %get-tuple-element.7) | copy-start | bytes 786436
  188.1 4.6 %copy-start = (f32[512,128]{1,0:T(8,128)S(1)}, f32[512,128]{1,0:T(8,128)}, u32[]{:S(2)}) copy-start(f32[512,128]{1,0:T(8,128)} %get-tuple-element.8) | copy-start | bytes 786436

commit v4 on v2

--- a/solution.py
+++ b/solution.py
@@ -12,7 +12,7 @@
 E = 96
 ROWS = 768
 LN = 128
-ORDER = (0, 3, 1, 2)
+ORDER = (1, 2, 0, 3)
 
 
 def copy_to(src, dst, send_sem, recv_sem, dev):
@@ -33,11 +33,11 @@
 
 
 def kernel(
-    pat, wgt, g_in, p_in, d_in,
+    pat, wgt, g_hbm, p_hbm, d_hbm,
     x_out, id_out, den_out,
-    gbuf, gt, lsrc, lbuf, loth, lrel, acc, xs, xb, dsend, drecv, term, tpair, px, dh, dp,
+    g_in, p_in, d_in, gbuf, gt, lsrc, lbuf, loth, lrel, acc, xs, xb, dsend, drecv, way, term, tpair, px, dh, dp,
     a_s, a_r, gz_s, gz_r, gy_s, gy_r, gr_s, gr_r, gc_s, gc_r,
-    lp_s, lp_r, lm_s, lm_r, x_s, x_r, d_s, d_r, t_s, t_r, p_s, p_r, h_s, h_r, o_s,
+    lp_s, lp_r, lm_s, lm_r, x_s, x_r, d_s, d_r, t_s, t_r, p_s, p_r, h_s, h_r, k_s, k_r, o_s, i_s,
 ):
     pole = lax.axis_index("pole")
     r = lax.axis_index("row")
@@ -65,11 +65,19 @@
     partner = {"pole": 2 * xx + 1 - core}
     across = {"col": 4 * oth + y}
 
+    loads = [
+        pltpu.make_async_copy(src, dst, i_s.at[i])
+        for i, (src, dst) in enumerate(((g_hbm, g_in), (p_hbm, p_in), (d_hbm, d_in)))
+    ]
+    for load in loads:
+        load.start()
+
     bar = pltpu.get_barrier_semaphore()
     peers = [at_y(1), at_y(2), at_y(3), at_z(1), at_z(7), across, partner]
     peers += [at_row(d) for d in (1, 2, 3)] + [at_x(d) for d in (1, 2, 3)]
     for dev in peers:
         pl.semaphore_signal(bar, inc=1, device_id=dev, device_id_type=MESH)
+    loads[0].wait()
     pl.semaphore_wait(bar, len(peers))
 
     def gz(t):
@@ -77,6 +85,12 @@
 
     for t in (0, 1):
         gz(t).start()
+    for load in loads[1:]:
+        load.wait()
+
+    @pl.when((r == 0) | (r == 3))
+    def _():
+        drecv[1] = jnp.zeros((2, 512, LN), BF16)
 
     fine = r * 8 + c
     for k in range(8):
@@ -122,23 +136,24 @@
     def extra(j, d):
         return copy_to(loth.at[j], lrel.at[j], x_s.at[j], x_r.at[j], at_z(d))
 
+    def launch_far(j):
+        @pl.when(r == 2)
+        def _():
+            extra(j, 1).start()
+
+        @pl.when(r == 1)
+        def _():
+            extra(j, 7).start()
+
+        @pl.when(r == 3)
+        def _():
+            up(j, 0, loth.at[j], z).start()
+
+        @pl.when(r == 0)
+        def _():
+            down(j, 0, loth.at[j], z).start()
+
     def launch(j):
-        @pl.when(r == 2)
-        def _():
-            extra(j, 1).start()
-
-        @pl.when(r == 1)
-        def _():
-            extra(j, 7).start()
-
-        @pl.when(r == 3)
-        def _():
-            up(j, 0, loth.at[j], z).start()
-
-        @pl.when(r == 0)
-        def _():
-            down(j, 0, loth.at[j], z).start()
-
         @pl.when(r < 3)
         def _():
             up(j, 0, lbuf.at[j, z], z).start()
@@ -147,6 +162,8 @@
         def _():
             down(j, 0, lbuf.at[j, z], z).start()
 
+    for j in range(4):
+        launch_far(j)
     for j in (0, 1):
         launch(j)
 
@@ -204,11 +221,10 @@
             extra(j, 7).wait_recv()
             down(j, 1, lrel.at[j], 4 * h + 1).start()
 
-    def relay_from(j, d):
+    def relay_up(j, d, live=True):
         zp = lax.rem(z + 7 - d, 8)
-        zm = lax.rem(z + 1 + d, 8)
-
-        @pl.when(d < r + 2)
+
+        @pl.when((d < r + 2) & live)
         def _():
             up(j, d, lbuf.at[j, zp], zp).wait_recv()
 
@@ -217,7 +233,10 @@
                 def _():
                     up(j, d + 1, lbuf.at[j, zp], zp).start()
 
-        @pl.when(d < 5 - r)
+    def relay_down(j, d, live=True):
+        zm = lax.rem(z + 1 + d, 8)
+
+        @pl.when((d < 5 - r) & live)
         def _():
             down(j, d, lbuf.at[j, zm], zm).wait_recv()
 
@@ -226,11 +245,12 @@
                 def _():
                     down(j, d + 1, lbuf.at[j, zm], zm).start()
 
-    def compute_from(j, d):
+    def compute_up(j, d):
         @pl.when(d < r + 2)
         def _():
             compute(j, j, lax.rem(z + 7 - d, 8))
 
+    def compute_down(j, d):
         @pl.when(d < 5 - r)
         def _():
             compute(j, j, lax.rem(z + 1 + d, 8))
@@ -259,66 +279,153 @@
 
         out_copy(j).start()
 
-    def diag(ja, jb):
-        low = lbuf[ja, r].reshape(4 * E, 2 * LN)
-        high = lbuf[ja, 4 + r].reshape(4 * E, 2 * LN)
-        both = dot(low, xb[jb, :4 * E], (0, 0)) + dot(high, xb[jb, 4 * E:], (0, 0))
-        lo = ORDER[ja] * LN
-        dsend[ORDER[jb], 0, lo:lo + LN] = (both[:LN, :LN] - both[LN:, LN:]).astype(BF16)
-        dsend[ORDER[jb], 1, lo:lo + LN] = (both[:LN, LN:] + both[LN:, :LN]).astype(BF16)
+    def diag(jb, start=0, stop=4):
+        @pl.loop(start, stop)
+        def _(ja):
+            low = lbuf[ja, r].reshape(4 * E, 2 * LN)
+            high = lbuf[ja, 4 + r].reshape(4 * E, 2 * LN)
+            both = dot(low, xb[jb, :4 * E], (0, 0)) + dot(high, xb[jb, 4 * E:], (0, 0))
+            rows = pl.ds(pl.multiple_of(ja * LN, LN), LN)
+            dsend[ORDER[jb], 0, rows, :] = (both[:LN, :LN] - both[LN:, LN:]).astype(BF16)
+            dsend[ORDER[jb], 1, rows, :] = (both[:LN, LN:] + both[LN:, :LN]).astype(BF16)
 
     for d in range(5):
         for j in (0, 1):
             if d == 0:
                 edge(j)
-            relay_from(j, d)
+            relay_up(j, d)
+            relay_down(j, d)
         if d == 2:
             for j in (2, 3):
                 launch(j)
-    for t in (0, 1):
-        for d in (1, 3, 2):
-            gc(d, t).wait_recv()
-    turn(oth)
+                edge(j)
+            for i in (0, 1):
+                for j in (2, 3):
+                    relay_up(j, i, r == 0)
+                    relay_down(j, i, r == 3)
+    def share(j, part):
+        own = ORDER[j]
+        d = lax.rem(own + 4 - r, 4) - 1
+        slot = jnp.maximum(d, 0)
+        rows = pl.ds(part * 2 * LN, 2 * LN)
+        return copy_to(
+            dsend.at[own, :, rows], drecv.at[slot, :, rows], d_s.at[slot, part], d_r.at[slot, part], {"row": own}
+        )
+
+    def give(j, part):
+        @pl.when(r != ORDER[j])
+        def _():
+            share(j, part).start()
+
+    def give_both(j):
+        share(j, 0).start()
+        share(j, 1).start()
+
     for d in range(5):
-        for j in (2, 3):
-            if d == 0:
-                edge(j)
-            relay_from(j, d)
-            if d == 0:
-                first(j)
-            compute_from(j, d)
-        if d < 2:
-            first(d)
-            compute_rest(d)
-            finish(d, d)
-    finish(2, 2)
-    finish(3, 3)
-
-    for jb in range(4):
-        for ja in range(4):
-            diag(ja, jb)
-
-    def share(d):
+        relay_up(2, d, r > 0)
+        relay_down(3, d, r < 3)
+        if d > 0:
+            relay_up(3, d - 1, r > 0)
+            relay_down(2, d - 1, r < 3)
+        if d == 0:
+            continue
+        if d == 1:
+            for t in (0, 1):
+                for i in (1, 3, 2):
+                    gc(i, t).wait_recv()
+            turn(oth)
+            first(2)
+            first(3)
+            compute_up(2, 0)
+            compute_down(3, 0)
+        compute_up(2, d)
+        compute_down(3, d)
+        compute_up(3, d - 1)
+        compute_down(2, d - 1)
+        if d < 3:
+            first(d - 1)
+            compute_rest(d - 1)
+            finish(d - 1, d - 1)
+        if d == 2:
+            diag(0, 0, 2)
+            diag(1, 0, 2)
+            give(0, 0)
+            give(1, 0)
+        if d == 4:
+            diag(0, 2, 4)
+            diag(1, 2, 4)
+            give(0, 1)
+            give(1, 1)
+
+    @pl.when(r > 0)
+    def _():
+        finish(2, 2)
+        diag(2)
+
+    @pl.when(r < 3)
+    def _():
+        finish(3, 3)
+        diag(3)
+
+    def meet(own):
+        return copy_to(dsend.at[own], way, k_s, k_r, {"row": 3 - r})
+
+    def pass_on(own, j):
+        meet(3 - own).start()
+        meet(own).wait_recv()
+        for t in (0, 1):
+            dsend[own, t] = (dsend[own, t].astype(F32) + way[t].astype(F32)).astype(BF16)
+        give_both(j)
+
+    @pl.when(r == 1)
+    def _():
+        pass_on(0, 2)
+
+    @pl.when(r == 2)
+    def _():
+        pass_on(3, 3)
+
+    @pl.when(r == 3)
+    def _():
+        give_both(2)
+        relay_up(3, 4)
+        compute_up(3, 4)
+        finish(3, 3)
+        diag(3)
+
+    @pl.when(r == 0)
+    def _():
+        give_both(3)
+        relay_down(2, 4)
+        compute_down(2, 4)
+        finish(2, 2)
+        diag(2)
+
+    def got(d, part):
+        rows = pl.ds(part * 2 * LN, 2 * LN)
         return copy_to(
-            dsend.at[lax.rem(r + d, 4)], drecv.at[d - 1], d_s.at[d - 1], d_r.at[d - 1], at_row(d)
+            dsend.at[r, :, rows], drecv.at[d, :, rows], d_s.at[d, part], d_r.at[d, part], partner
         )
 
-    for d in (1, 2, 3):
-        share(d).start()
-    for d in (1, 2, 3):
-        share(d).wait_recv()
-
-    def full(t):
-        got = dsend[r, t].astype(F32)
-        for d in range(3):
-            got += drecv[d, t].astype(F32)
-        return d_in[0, t].astype(F32) - got
-
-    re = full(0)
-    im = full(1)
-    id_out[0, 0] = re.astype(BF16)
-    id_out[0, 1] = im.astype(BF16)
-    term[...] = wgt[0, 0] * im + wgt[0, 1] * re
+    for part in (0, 1):
+        got(0, part).wait_recv()
+        got(2, part).wait_recv()
+
+        @pl.when((r == 1) | (r == 2))
+        def _():
+            got(1, part).wait_recv()
+
+    for j in range(4):
+        rows = pl.ds(j * LN, LN)
+        cols = pl.ds(ORDER[j] * LN, LN)
+        part = []
+        for t in (0, 1):
+            sum_ = dsend[r, t, rows, :].astype(F32)
+            for d in range(3):
+                sum_ += drecv[d, t, rows, :].astype(F32)
+            part.append(d_in[0, t, cols, :].astype(F32) - sum_)
+            id_out[0, t, cols, :] = part[t].astype(BF16)
+        term[cols, :] = wgt[0, 0] * part[1] + wgt[0, 1] * part[0]
 
     mine = pl.ds(pl.multiple_of(core * 256, 256), 256)
     other = pl.ds(pl.multiple_of((1 - core) * 256, 256), 256)
@@ -352,8 +459,26 @@
         for d in (1, 2, 3):
             gc(d, t).wait_send()
             to_col(d, t).wait_send()
+    for j in (0, 1):
+        @pl.when(r != ORDER[j])
+        def _():
+            for part in (0, 1):
+                share(j, part).wait_send()
+
+    for part in (0, 1):
+        @pl.when((r == 1) | (r == 3))
+        def _():
+            share(2, part).wait_send()
+
+        @pl.when((r == 0) | (r == 2))
+        def _():
+            share(3, part).wait_send()
+
+    @pl.when((r == 1) | (r == 2))
+    def _():
+        meet(0).wait_send()
+
     for d in (1, 2, 3):
-        share(d).wait_send()
         along(d).wait_send()
     pair.wait_send()
     swap.wait_send()
@@ -380,9 +505,10 @@
 
 def body(anc_inverse, panel, pattern, diag_inverse, pole_weights):
     vmem = pl.BlockSpec(memory_space=pltpu.VMEM)
+    hbm = pl.BlockSpec(memory_space=pl.ANY)
     smem = pl.BlockSpec(memory_space=pltpu.SMEM)
     dma = pltpu.SemaphoreType.DMA
-    sems = [(3, 2), (2,), (2, 2), (2,), (3, 2), (4, 5), (4, 5), (4,), (3,), None, (3,), None]
+    sems = [(3, 2), (2,), (2, 2), (2,), (3, 2), (4, 5), (4, 5), (4,), (3, 2), None, (3,), None, None]
     pairs = []
     for shape in sems:
         one = dma if shape is None else dma(shape)
@@ -394,9 +520,12 @@
             jax.ShapeDtypeStruct((1, 2, 512, LN), BF16),
             jax.ShapeDtypeStruct((512, LN), F32),
         ),
-        in_specs=[smem, smem, vmem, vmem, vmem],
-        out_specs=(pl.BlockSpec(memory_space=pl.ANY), vmem, vmem),
+        in_specs=[smem, smem, hbm, hbm, hbm],
+        out_specs=(hbm, vmem, vmem),
         scratch_shapes=[
+            pltpu.VMEM((1, 2, 4, E, ROWS), BF16),
+            pltpu.VMEM((1, 2, E, 4096), BF16),
+            pltpu.VMEM((1, 2, 512, LN), BF16),
             pltpu.VMEM((2, 2, 4, 4, E, ROWS), BF16),
             pltpu.VMEM((8, 2, ROWS, 4 * E), BF16),
             pltpu.VMEM((8, 4, E, 2 * LN), BF16),
@@ -408,6 +537,7 @@
             pltpu.VMEM((4, ROWS, 2 * LN), BF16),
             pltpu.VMEM((4, 2, 512, LN), BF16),
             pltpu.VMEM((3, 2, 512, LN), BF16),
+            pltpu.VMEM((2, 512, LN), BF16),
             pltpu.VMEM((512, LN), F32),
             pltpu.VMEM((256, LN), F32),
             pltpu.VMEM((4, 256, LN), BF16),
@@ -415,6 +545,7 @@
             pltpu.VMEM((256, LN), F32),
             *pairs,
             dma((4,)),
+            dma((3,)),
         ],
         compiler_params=pltpu.CompilerParams(
             collective_id=0, has_side_effects=True, vmem_limit_bytes=60 * 1024 * 1024

time: 204 us -> 191 us (0.936); the launches traced: 203 us -> 187 us
  Pallas kernels: 197 us -> 181 us
    pallas_call x1, Pallas kernels: 197 us -> 181 us  [body(): pl.pallas_call(kernel, out_shape=(jax.ShapeDtypeStruct((1, 2, ROWS, 512),...]
where the time goes in v4:
time: 191 us; the launch traced here: 187 us
  Pallas kernels  181 us (95%)
  local copies, waits for them, and re-layouts  5.33 us (3%)
    pallas_call x1, Pallas kernels, body(): pl.pallas_call(kernel, out_shape=(jax.ShapeDtypeStruct((1, 2, ROWS, 512),...  181 us
    unnamed x7, local copies, waits for them, and re-layouts  5.33 us

profile of v4, /device:TPU:105, one launch (start us, length us, event | category | flops | bytes accessed | tf_op | source)
XLA Modules:
  0.0 187.1 jit_solution(840886274739919361)
XLA Ops:
  0.6 181.1 %shard_map.76 = (f32[1,2,768,512]{3,2,1,0:T(8,128)}, bf16[1,2,512,128]{3,2,1,0:T(8,128)(2,1)}, f32[512,128]{1,0:T(8,128)}) custom-call(s32[8,32]{1,0:T(8,128)} %bitcast.1, f32[1,2]{1,0:T(1,128)} %wgt.1, bf16[1,2,4,96,768]{4,3,2,1,0:T(8,128)(2,1)} %g_hbm.1, bf16[1,2,96,4096]{3,2,1,0:T(8,128)(2,1)} %p_hbm.1, bf16[1,2,512,128]{3,2,1,0:T(8,128)(2,1)} %d_hbm.1), custom_call_target="tpu_custom_call" | custom-call | tf_op jit(solution)/shard_map/pallas_call | solution.py:516
  181.7 0.0 copy-start.1
  181.8 0.0 copy-start
  181.8 3.9 %copy.11 = f32[1,2,768,512]{3,2,1,0:T(8,128)} copy(f32[1,2,768,512]{3,2,1,0:T(8,128)} %get-tuple-element.6) | data formatting | bytes 6291456
  185.7 0.0 copy-done.1
  185.7 0.7 copy.12
  186.4 0.0 copy-done
  186.4 0.7 copy.13
Async XLA Ops:
  181.7 3.9 %copy-start.1 = (bf16[1,2,512,128]{3,2,1,0:T(8,128)(2,1)S(1)}, bf16[1,2,512,128]{3,2,1,0:T(8,128)(2,1)}, u32[]{:S(2)}) copy-start(bf16[1,2,512,128]{3,2,1,0:T(8,128)(2,1)} %get-tuple-element.7) | copy-start | bytes 786436
  181.8 4.6 %copy-start = (f32[512,128]{1,0:T(8,128)S(1)}, f32[512,128]{1,0:T(8,128)}, u32[]{:S(2)}) copy-start(f32[512,128]{1,0:T(8,128)} %get-tuple-element.8) | copy-start | bytes 786436

commit v5 on v4

--- a/solution.py
+++ b/solution.py
@@ -35,7 +35,7 @@
 def kernel(
     pat, wgt, g_hbm, p_hbm, d_hbm,
     x_out, id_out, den_out,
-    g_in, p_in, d_in, gbuf, gt, lsrc, lbuf, loth, lrel, acc, xs, xb, dsend, drecv, way, term, tpair, px, dh, dp,
+    g_in, p_in, d_in, gbuf, gt, lsrc, lbuf, loth, lrel, acc, xb, dsend, drecv, way, term, tpair, px, dh, dp,
     a_s, a_r, gz_s, gz_r, gy_s, gy_r, gr_s, gr_r, gc_s, gc_r,
     lp_s, lp_r, lm_s, lm_r, x_s, x_r, d_s, d_r, t_s, t_r, p_s, p_r, h_s, h_r, k_s, k_r, o_s, i_s,
 ):
@@ -262,22 +262,24 @@
 
     def out_copy(j):
         cols = pl.ds(ORDER[j] * LN, LN)
-        return pltpu.make_async_copy(xs.at[:, :, cols], x_out.at[0, :, :, cols], o_s.at[j])
+        return [
+            pltpu.make_async_copy(
+                xb.at[j, :, pl.ds(t * LN, LN)], x_out.at[0, t, :, cols], o_s.at[j, t]
+            )
+            for t in (0, 1)
+        ]
 
     def finish(slot, j):
-        lo = ORDER[j] * LN
-
         @pl.loop(0, 8)
         def _(b):
             rows = pl.ds(b * E, E)
             re = acc[slot, 1, rows, LN:] - acc[slot, 0, rows, :LN]
             im = -(acc[slot, 0, rows, LN:] + acc[slot, 1, rows, :LN])
-            xs[0, rows, lo:lo + LN] = re
-            xs[1, rows, lo:lo + LN] = im
             xb[j, rows, :LN] = re.astype(BF16)
             xb[j, rows, LN:] = im.astype(BF16)
 
-        out_copy(j).start()
+        for one in out_copy(j):
+            one.start()
 
     def diag(jb, start=0, stop=4):
         @pl.loop(start, stop)
@@ -500,7 +502,8 @@
                 down(j, i, lbuf.at[j, z], z).wait_send()
 
     for j in range(4):
-        out_copy(j).wait()
+        for one in out_copy(j):
+            one.wait()
 
 
 def body(anc_inverse, panel, pattern, diag_inverse, pole_weights):
@@ -513,10 +516,10 @@
     for shape in sems:
         one = dma if shape is None else dma(shape)
         pairs += [one, one]
-    return pl.pallas_call(
+    inv_panel, inv_diag, density = pl.pallas_call(
         kernel,
         out_shape=(
-            jax.ShapeDtypeStruct((1, 2, ROWS, 512), F32),
+            jax.ShapeDtypeStruct((1, 2, ROWS, 512), BF16),
             jax.ShapeDtypeStruct((1, 2, 512, LN), BF16),
             jax.ShapeDtypeStruct((512, LN), F32),
         ),
@@ -533,7 +536,6 @@
             pltpu.VMEM((4, 4, E, 2 * LN), BF16),
             pltpu.VMEM((4, 4, E, 2 * LN), BF16),
             pltpu.VMEM((4, 2, ROWS, 2 * LN), F32),
-            pltpu.VMEM((2, ROWS, 512), F32),
             pltpu.VMEM((4, ROWS, 2 * LN), BF16),
             pltpu.VMEM((4, 2, 512, LN), BF16),
             pltpu.VMEM((3, 2, 512, LN), BF16),
@@ -544,13 +546,14 @@
             pltpu.VMEM((256, LN), F32),
             pltpu.VMEM((256, LN), F32),
             *pairs,
-            dma((4,)),
+            dma((4, 2)),
             dma((3,)),
         ],
         compiler_params=pltpu.CompilerParams(
             collective_id=0, has_side_effects=True, vmem_limit_bytes=60 * 1024 * 1024
         ),
     )(pattern.T, pole_weights, anc_inverse, panel, diag_inverse)
+    return inv_panel.astype(F32), inv_diag, density
 
 
 def solution(mesh):

time: 191 us -> 191 us (level)
  local copies, waits for them, and re-layouts: 5.33 us -> 1.41 us
  other arithmetic: 0 us -> 3.57 us
    unnamed x7 -> x6, local copies, waits for them, and re-layouts: 5.33 us -> 1.41 us
    convert_element_type x0 -> x1, other arithmetic: none -> 3.57 us  [body(): return (inv_panel.astype(F32), inv_diag, density)]
where the time goes in v5:
time: 191 us; the launch traced here: 187 us
  Pallas kernels  181 us (95%)
  other arithmetic  3.57 us (2%)
    pallas_call x1, Pallas kernels, body(): pl.pallas_call(kernel, out_shape=(jax.ShapeDtypeStruct((1, 2, ROWS, 512),...  181 us

profile of v5, /device:TPU:105, one launch (start us, length us, event | category | flops | bytes accessed | tf_op | source)
XLA Modules:
  0.0 186.8 jit_solution(99678451447308045)
XLA Ops:
  0.6 181.1 %shard_map.76 = (bf16[1,2,768,512]{3,2,1,0:T(8,128)(2,1)}, bf16[1,2,512,128]{3,2,1,0:T(8,128)(2,1)}, f32[512,128]{1,0:T(8,128)}) custom-call(s32[8,32]{1,0:T(8,128)} %bitcast.1, f32[1,2]{1,0:T(1,128)} %wgt.1, bf16[1,2,4,96,768]{4,3,2,1,0:T(8,128)(2,1)} %g_hbm.1, bf16[1,2,96,4096]{3,2,1,0:T(8,128)(2,1)} %p_hbm.1, bf16[1,2,512,128]{3,2,1,0:T(8,128)(2,1)} %d_hbm.1), custom_call_target="tpu_custom_call" | custom-call | tf_op jit(solution)/shard_map/pallas_call | solution.py:519
  181.8 0.0 copy-start.1
  181.8 0.0 copy-start
  181.8 3.6 %convert_element_type.3 = f32[1,2,768,512]{3,2,1,0:T(8,128)} convert(bf16[1,2,768,512]{3,2,1,0:T(8,128)(2,1)} %get-tuple-element.6) | non-fusion elementwise | flops 786432 | bytes 4718592 | tf_op jit(solution)/shard_map/convert_element_type | solution.py:556
  185.4 0.0 copy-done.1
  185.4 0.7 copy.10
  186.1 0.0 copy-done
  186.1 0.7 copy.11
Async XLA Ops:
  181.8 3.6 %copy-start.1 = (bf16[1,2,512,128]{3,2,1,0:T(8,128)(2,1)S(1)}, bf16[1,2,512,128]{3,2,1,0:T(8,128)(2,1)}, u32[]{:S(2)}) copy-start(bf16[1,2,512,128]{3,2,1,0:T(8,128)(2,1)} %get-tuple-element.13) | copy-start | bytes 786436
  181.8 4.3 %copy-start = (f32[512,128]{1,0:T(8,128)S(1)}, f32[512,128]{1,0:T(8,128)}, u32[]{:S(2)}) copy-start(f32[512,128]{1,0:T(8,128)} %get-tuple-element.14) | copy-start | bytes 786436
